TPU v7x, 256 devices: a whole 4x4x8 slice. The times are simulated.
256 devices in a mesh: space: 64 (over y, z, core), col: 4 (over x).
Axes of the slice: x: 4, y: 4, z: 8, core: 2. Of those that a mesh axis runs over, the one named last changes fastest.
Arguments:
- first_snaps: float32 [458752, 512], P(('space', 'col')), may hold values from -7200 to 7200, as said below
- next_snaps: float32 [458752, 512], P(('space', 'col')), may hold values from -24 to 24
Outputs:
- reduced_operator: float32 [512, 512], replicated
- mode_basis: float32 [458752, 512], P(('space', 'col'))
Inputs may be any that keep to these rules, and one draw needn't show every extreme that they name: `first_snaps`: Real-valued snapshots; the columns are linearly independent.
All inputs are finite; a program needn't handle non-finite values.
Results may differ from a plain program's by a relative error of at most 0.00017.
Values sent between devices are 32-bit elements; how exact they have to be, the bound alone decides.
A program may use at most 64 MiB of HBM per device.

v0:
```python
import functools
import math

import jax
import jax.numpy as jnp
from jax import lax
from jax.experimental import pallas as pl
from jax.experimental.pallas import tpu as pltpu
from jax.sharding import Mesh
from jax.sharding import PartitionSpec as P

AXES = ("y", "z", "c", "x")
MESH = pl.DeviceIdType.MESH
K = 512
NB = 128
F32, BF16 = jnp.float32, jnp.bfloat16
T0 = (((0,), (0,)), ((), ()))
NN = (((1,), (0,)), ((), ()))
NT = (((1,), (1,)), ((), ()))
UPPER = [(i, j) for i in range(4) for j in range(i, 4)]


def split2(x):
    hi = x.astype(BF16)
    return hi, (x - hi.astype(F32)).astype(BF16)


def split3(x):
    hi = x.astype(BF16)
    rest = x - hi.astype(F32)
    mid = rest.astype(BF16)
    return hi, mid, (rest - mid.astype(F32)).astype(BF16)


def mm(a, b, dims):
    return lax.dot_general(a, b, dims, preferred_element_type=F32)


def lane_splat(v, lane):
    return jnp.broadcast_to(v[:, lane : lane + 1], v.shape)


def row_splat(v, row):
    return jnp.broadcast_to(v[row : row + 1, :], v.shape)


def eliminate_block(w, out):
    sub = lax.broadcasted_iota(jnp.int32, (8, NB), 0)
    for t in range(NB // 8):
        r0 = 8 * t
        pa, pb = w[r0 : r0 + 8, :NB], w[r0 : r0 + 8, NB:]
        s = [lane_splat(pa, r0 + j) for j in range(8)]
        rs, uas, ubs, ums = [], [], [], []
        for j in range(8):
            r = lax.rsqrt(row_splat(s[j], j))
            low = jnp.where(sub > j, s[j] * r, 0.0)
            ua, ub = row_splat(pa, j) * r, row_splat(pb, j) * r
            um = {m: row_splat(s[m], j) * r for m in range(j + 1, 8)}
            for m in um:
                s[m] = s[m] - low * um[m]
            pa, pb = pa - low * ua, pb - low * ub
            out[r0 + j : r0 + j + 1, :] = ub[0:1, :]
            rs.append(r), uas.append(ua), ubs.append(ub), ums.append(um)
        for g in range(t + 1, NB // 8):
            rows = slice(8 * g, 8 * g + 8)
            wa, wb = w[rows, :NB], w[rows, NB:]
            sg = [lane_splat(wa, r0 + j) for j in range(8)]
            for j in range(8):
                low = sg[j] * rs[j]
                for m in range(j + 1, 8):
                    sg[m] = sg[m] - low * ums[j][m]
                wa, wb = wa - low * uas[j], wb - low * ubs[j]
            w[rows, :NB], w[rows, NB:] = wa, wb


def dot6(a3, b3, dims):
    ca, cb = dims[0][0][0], dims[0][1][0]
    ah, am, al = a3
    bh, bm, bl = b3
    left = jnp.concatenate([ah, ah, am, ah, al, am], axis=ca)
    right = jnp.concatenate([bh, bm, bh, bl, bh, bm], axis=cb)
    return mm(left, right, dims)


def invert_factor(z, w, m11, m):
    eye = jnp.where(
        lax.broadcasted_iota(jnp.int32, (NB, NB), 0) == lax.broadcasted_iota(jnp.int32, (NB, NB), 1), 1.0, 0.0
    ).astype(F32)
    for kb in range(4):
        c0, c1 = kb * NB, (kb + 1) * NB
        rows = slice(c0, c1)
        w[:, :NB] = z[rows, c0:c1]
        w[:, NB:] = eye
        eliminate_block(w, m11)
        inv = m11[...]
        m[rows, c0:c1] = inv
        inv3 = split3(inv)
        if kb > 0:
            left = dot6(inv3, split3(z[rows, :c0]), NN)
            m[rows, :c0] = left
            left3 = split3(left)
        if kb < 3:
            m[rows, c1:] = jnp.zeros((NB, K - c1), F32)
            right3 = split3(dot6(inv3, split3(z[rows, c1:]), NN))
            z[c1:, c1:] = z[c1:, c1:] - dot6(right3, right3, T0)
            z[c1:, c0:c1] = -dot6(right3, inv3, T0)
            if kb > 0:
                z[c1:, :c0] = z[c1:, :c0] - dot6(right3, left3, T0)


def finish_kernel(scale, g_ref, c_ref, y_ref, red_ref, mode_ref, z, w, m11, m, mh, ml):
    @pl.when(pl.program_id(0) == 0)
    def _():
        for b, (i, j) in enumerate(UPPER):
            z[i * NB : (i + 1) * NB, j * NB : (j + 1) * NB] = g_ref[b // 5, (b % 5) * NB : (b % 5 + 1) * NB, :]
        invert_factor(z, w, m11, m)
        hi, lo = split2(m[...])
        mh[...], ml[...] = hi, lo
        for b in range(16):
            i, j = b // 4, b % 4
            z[i * NB : (i + 1) * NB, j * NB : (j + 1) * NB] = c_ref[b // 8, (b % 8) * NB : (b % 8 + 1) * NB, :]
        ch, cl = split2(z[...])
        lh, ll = split2(mm(hi, ch, NN) + mm(hi, cl, NN) + mm(lo, ch, NN))
        red_ref[...] = (mm(lh, hi, NT) + mm(lh, lo, NT) + mm(ll, hi, NT)) * scale

    yh, yl = split2(y_ref[...])
    for n, k1 in ((0, 256), (256, 512)):
        ph, plo = mh[n : n + 256, :k1], ml[n : n + 256, :k1]
        ah, al = yh[:, :k1], yl[:, :k1]
        mode_ref[:, n : n + 256] = (mm(ah, ph, NT) + mm(ah, plo, NT) + mm(al, ph, NT)) * scale


def finish(gram, cross, y, scale):
    rows = y.shape[0]
    step = rows // 4
    whole = lambda *shape: pl.BlockSpec(shape, lambda i: (0,) * len(shape))
    return pl.pallas_call(
        functools.partial(finish_kernel, scale),
        grid=(4,),
        out_shape=(jax.ShapeDtypeStruct((K, K), F32), jax.ShapeDtypeStruct((rows, K), F32)),
        in_specs=[whole(*gram.shape), whole(*cross.shape), pl.BlockSpec((step, K), lambda i: (i, 0))],
        out_specs=(whole(K, K), pl.BlockSpec((step, K), lambda i: (i, 0))),
        scratch_shapes=[
            pltpu.VMEM((K, K), F32),
            pltpu.VMEM((NB, 2 * NB), F32),
            pltpu.VMEM((NB, NB), F32),
            pltpu.VMEM((K, K), F32),
            pltpu.VMEM((K, K), BF16),
            pltpu.VMEM((K, K), BF16),
        ],
        compiler_params=pltpu.CompilerParams(vmem_limit_bytes=60 << 20),
        name="factor_and_modes",
    )(gram, cross, y)


GP, CP = 40, 64


def to_blocks(ref, first, value):
    per = ref.shape[1] // NB
    for n in range(value.shape[1] // NB):
        b = first + n
        ref[b // per, (b % per) * NB : (b % per + 1) * NB, :] = value[:, n * NB : (n + 1) * NB]


def sums_kernel(x_hbm, y_hbm, g_out, c_out, xv, yv, xh, xl, yh, yl, gloc, cloc, gpart, cpart, gsum, csum, gxy, cxy, gz, cz,
                gred, in_sem, d_send, d_recv, xy_send, xy_recv, z_send, z_recv, ag_send, ag_recv, e_send, e_recv, c_sem):
    my, mz, mc, mx = [lax.axis_index(a) for a in AXES]
    oc = 1 - mc
    me = my * 4 + mx
    rows = xv.shape[0]
    chunks = rows // 256

    loads = []
    for n, (src, dst) in enumerate(((x_hbm, xv), (y_hbm, yv))):
        for i in range(chunks):
            part = pl.ds(i * 256, 256)
            loads.append(pltpu.make_async_copy(src.at[part], dst.at[part], in_sem.at[n * chunks + i]))
    for load in loads:
        load.start()

    plane = [(dy, dx) for dy in range(4) for dx in range(4)][1:]

    def in_plane(dy, dx):
        return lax.rem(my + dy, 4), lax.rem(mx + dx, 4)

    def along_z(dz):
        return lax.rem(mz + dz, 8)

    barrier = pltpu.get_barrier_semaphore()
    pl.semaphore_signal(barrier, inc=1, device_id=(my, mz, oc, mx), device_id_type=MESH)
    for dy, dx in plane:
        py, px = in_plane(dy, dx)
        pl.semaphore_signal(barrier, inc=1, device_id=(py, mz, mc, px), device_id_type=MESH)
    for dz in range(1, 8):
        pl.semaphore_signal(barrier, inc=1, device_id=(my, along_z(dz), mc, mx), device_id_type=MESH)

    def partner(src, dst, n, sems):
        return pltpu.make_async_remote_copy(src, dst, sems[0].at[n], sems[1].at[n], device_id=(my, mz, oc, mx), device_id_type=MESH)

    def piece(ref, who, size):
        return ref.at[pl.ds(pl.multiple_of(who * size, 8), size), :]

    def scatter_plane(part, landing, size, n):
        out = []
        for k, (dy, dx) in enumerate(plane):
            py, px = in_plane(dy, dx)
            out.append(pltpu.make_async_remote_copy(
                piece(part, py * 4 + px, size), landing.at[k], xy_send.at[n, k], xy_recv.at[n, k],
                device_id=(py, mz, mc, px), device_id_type=MESH))
        return out

    def gather_plane(mine, whole, size, n):
        out = []
        for k, (dy, dx) in enumerate(plane):
            py, px = in_plane(dy, dx)
            out.append(pltpu.make_async_remote_copy(
                mine, piece(whole, me, size), ag_send.at[n, k], ag_recv.at[n, k],
                device_id=(py, mz, mc, px), device_id_type=MESH))
        return out

    def start(copies):
        for c in copies:
            c.start()

    def wait(copies):
        for c in copies:
            c.wait()

    for i in range(chunks):
        loads[i].wait()
        part = slice(i * 256, i * 256 + 256)
        xh[part, :], xl[part, :] = split2(xv[part, :])
    left, right = slice(0, 256), slice(256, 512)
    for cols, firsts in ((left, (0, 4)), (right, (7, 9))):
        h, l = xh[:, cols], xl[:, cols]
        hl = mm(h, l, T0)
        g = mm(h, h, T0) + mm(l, l, T0) + hl + hl.T
        to_blocks(gloc, firsts[0], g[:NB])
        to_blocks(gloc, firsts[1], g[NB:, NB:])
    h, l = xh[:, left], xl[:, left]
    h2, l2 = xh[:, right], xl[:, right]
    g = mm(h, h2, T0) + mm(h, l2, T0) + mm(l, h2, T0) + mm(l, l2, T0)
    to_blocks(gloc, 2, g[:NB])
    to_blocks(gloc, 5, g[NB:])

    pl.semaphore_wait(barrier, 1 + len(plane) + 7)
    g_d = partner(gloc.at[oc], gpart, 0, (d_send, d_recv))
    g_d.start()

    for i in range(chunks):
        loads[chunks + i].wait()
        part = slice(i * 256, i * 256 + 256)
        yh[part, :], yl[part, :] = split2(yv[part, :])
    for i in range(4):
        h, l = xh[:, i * NB : (i + 1) * NB], xl[:, i * NB : (i + 1) * NB]
        to_blocks(cloc, 4 * i, mm(h, yh[...], T0) + mm(h, yl[...], T0) + mm(l, yh[...], T0))
    c_d = partner(cloc.at[oc], cpart, 1, (d_send, d_recv))
    c_d.start()

    g_d.wait()
    gsum[...] = gloc[mc] + gpart[...]
    g_xy = scatter_plane(gsum, gxy, GP, 0)
    start(g_xy)
    c_d.wait()
    csum[...] = cloc[mc] + cpart[...]
    c_xy = scatter_plane(csum, cxy, CP, 1)
    start(c_xy)

    wait(g_xy)
    total = gsum[pl.ds(pl.multiple_of(me * GP, 8), GP), :]
    for k in range(15):
        total = total + gxy[k]
    gred[...] = total
    gz[mz] = total
    g_z = [pltpu.make_async_remote_copy(gred, gz.at[mz], z_send.at[0, k], z_recv.at[0, k],
                                        device_id=(my, along_z(k + 1), mc, mx), device_id_type=MESH) for k in range(7)]
    start(g_z)

    wait(c_xy)
    total = csum[pl.ds(pl.multiple_of(me * CP, 8), CP), :]
    for k in range(15):
        total = total + cxy[k]
    csum[0:CP, :] = total
    c_z = [pltpu.make_async_remote_copy(piece(csum, along_z(k + 1), 8), cz.at[k], z_send.at[1, k], z_recv.at[1, k],
                                        device_id=(my, along_z(k + 1), mc, mx), device_id_type=MESH) for k in range(7)]
    start(c_z)

    wait(g_z)
    total = gz[0]
    for k in range(1, 8):
        total = total + gz[k]
    g_out[mc, pl.ds(pl.multiple_of(me * GP, 8), GP), :] = total
    g_ag = gather_plane(piece(g_out.at[mc], me, GP), g_out.at[mc], GP, 0)
    start(g_ag)

    wait(c_z)
    total = csum[pl.ds(pl.multiple_of(mz * 8, 8), 8), :]
    for k in range(7):
        total = total + cz[k]
    mine = pl.multiple_of(me * CP, 8)
    c_out[mc, pl.ds(mine + pl.multiple_of(mz * 8, 8), 8), :] = total
    src = c_out.at[mc, pl.ds(mine + pl.multiple_of(mz * 8, 8), 8), :]
    c_zg = [pltpu.make_async_remote_copy(src, src, z_send.at[2, k], z_recv.at[2, k],
                                         device_id=(my, along_z(k + 1), mc, mx), device_id_type=MESH) for k in range(7)]
    start(c_zg)

    wait(g_ag)
    g_e = partner(g_out.at[mc], g_out.at[mc], 0, (e_send, e_recv))
    g_e.start()

    wait(c_zg)
    c_ag = gather_plane(piece(c_out.at[mc], me, CP), c_out.at[mc], CP, 1)
    start(c_ag)
    wait(c_ag)
    c_e = partner(c_out.at[mc], c_out.at[mc], 1, (e_send, e_recv))
    c_e.start()
    g_e.wait()
    c_e.wait()


def sums(x, y):
    rows = x.shape[0]
    chunks = rows // 256
    vm = pltpu.VMEM
    dma = pltpu.SemaphoreType.DMA
    return pl.pallas_call(
        sums_kernel,
        out_shape=(jax.ShapeDtypeStruct((2, 640, NB), F32), jax.ShapeDtypeStruct((2, 1024, NB), F32)),
        in_specs=[pl.BlockSpec(memory_space=pl.ANY)] * 2,
        out_specs=(pl.BlockSpec(memory_space=pltpu.VMEM),) * 2,
        scratch_shapes=[
            vm((rows, K), F32), vm((rows, K), F32),
            vm((rows, K), BF16), vm((rows, K), BF16), vm((rows, K), BF16), vm((rows, K), BF16),
            vm((2, 640, NB), F32), vm((2, 1024, NB), F32),
            vm((640, NB), F32), vm((1024, NB), F32), vm((640, NB), F32), vm((1024, NB), F32),
            vm((15, GP, NB), F32), vm((15, CP, NB), F32), vm((8, GP, NB), F32), vm((7, 8, NB), F32), vm((GP, NB), F32),
            dma((2 * chunks,)), dma((2,)), dma((2,)), dma((2, 15)), dma((2, 15)), dma((3, 7)), dma((3, 7)),
            dma((2, 15)), dma((2, 15)), dma((2,)), dma((2,)), dma(()),
        ],
        compiler_params=pltpu.CompilerParams(collective_id=0, has_side_effects=True, vmem_limit_bytes=60 << 20),
        name="products_and_sums",
    )(x, y)


def on_device(first_snaps, next_snaps):
    scale = math.sqrt(first_snaps.shape[0] * lax.axis_size(AXES))
    gram, cross = sums(first_snaps, next_snaps)
    return finish(gram, cross, next_snaps, scale)


def solution(mesh):
    finer = Mesh(mesh.devices.reshape(4, 8, 2, 4), AXES)
    spec = P(AXES, None)
    return jax.shard_map(
        on_device, mesh=finer, in_specs=(spec, spec), out_specs=(P(), spec), check_vma=False
    )
```

profile of v0, /device:TPU:1, one launch (start us, length us, event | category | flops | bytes accessed | tf_op | source)
XLA Modules:
  0.0 75.8 jit_solution(4911584522976031315)
XLA Ops:
  0.6 48.2 %products_and_sums.1 = (f32[2,640,128]{2,1,0:T(8,128)}, f32[2,1024,128]{2,1,0:T(8,128)}) custom-call(f32[1792,512]{1,0:T(8,128)} %x_hbm.1, f32[1792,512]{1,0:T(8,128)} %y_ref.1), custom_call_target="tpu_custom_call" | custom-call | tf_op jit(solution)/shard_map/products_and_sums/pallas_call | solution.py:327
  48.8 27.0 %factor_and_modes.1 = (f32[512,512]{1,0:T(8,128)}, f32[1792,512]{1,0:T(8,128)}) custom-call(f32[2,640,128]{2,1,0:T(8,128)} %get-tuple-element.4.g_ref, f32[2,1024,128]{2,1,0:T(8,128)} %get-tuple-element.5.c_ref, f32[1792,512]{1,0:T(8,128)} %y_ref.1), custom_call_target="tpu_custom_call" | custom-call | tf_op jit(solution)/shard_map/factor_and_modes/pallas_call | solution.py:137
where the time goes:
time: 75.9 us; the launch traced here: 75.8 us
  Pallas kernels  75.1 us (99%)
    pallas_call x1, Pallas kernels, sums(): pl.pallas_call(sums_kernel, out_shape=(jax.ShapeDtypeStruct((2, 640, NB),...  48.2 us
    pallas_call x1, Pallas kernels, finish(): pl.pallas_call(functools.partial(finish_kernel, scale), grid=(4,), out_sh...  27 us

commit v1 on v0

--- a/solution.py
+++ b/solution.py
@@ -82,39 +82,37 @@
     return mm(left, right, dims)
 
 
-def invert_factor(z, w, m11, m):
+def invert_factor(z, w, m11, m, between):
     eye = jnp.where(
         lax.broadcasted_iota(jnp.int32, (NB, NB), 0) == lax.broadcasted_iota(jnp.int32, (NB, NB), 1), 1.0, 0.0
     ).astype(F32)
-    for kb in range(4):
-        c0, c1 = kb * NB, (kb + 1) * NB
-        rows = slice(c0, c1)
-        w[:, :NB] = z[rows, c0:c1]
+    cols = lax.broadcasted_iota(jnp.int32, (NB, K), 1)
+    wide = lax.broadcasted_iota(jnp.int32, (K, K), 1)
+
+    def block_step(kb, carry):
+        between(kb)
+        c0 = pl.multiple_of(kb * NB, NB)
+        c1 = c0 + NB
+        rows = pl.ds(c0, NB)
+        w[:, :NB] = z[rows, rows]
         w[:, NB:] = eye
         eliminate_block(w, m11)
-        inv = m11[...]
-        m[rows, c0:c1] = inv
-        inv3 = split3(inv)
-        if kb > 0:
-            left = dot6(inv3, split3(z[rows, :c0]), NN)
-            m[rows, :c0] = left
-            left3 = split3(left)
-        if kb < 3:
-            m[rows, c1:] = jnp.zeros((NB, K - c1), F32)
-            right3 = split3(dot6(inv3, split3(z[rows, c1:]), NN))
-            z[c1:, c1:] = z[c1:, c1:] - dot6(right3, right3, T0)
-            z[c1:, c0:c1] = -dot6(right3, inv3, T0)
-            if kb > 0:
-                z[c1:, :c0] = z[c1:, :c0] - dot6(right3, left3, T0)
-
-
-def finish_kernel(scale, g_ref, c_ref, y_ref, red_ref, mode_ref, z, w, m11, m, mh, ml):
+        z[rows, rows] = eye
+        t = dot6(split3(m11[...]), split3(z[rows, :]), NN)
+        m[rows, :] = jnp.where(cols < c1, t, 0.0)
+        later = cols >= c1
+        t3 = split3(t)
+        update = dot6(split3(jnp.where(later, t, 0.0)), t3, T0)
+        z[...] = jnp.where((wide >= c0) & (wide < c1), 0.0, z[...]) - update
+        return carry
+
+    lax.fori_loop(0, K // NB, block_step, 0)
+
+
+def finish_kernel(scale, m_ref, c_ref, y_ref, red_ref, mode_ref, z, mh, ml):
     @pl.when(pl.program_id(0) == 0)
     def _():
-        for b, (i, j) in enumerate(UPPER):
-            z[i * NB : (i + 1) * NB, j * NB : (j + 1) * NB] = g_ref[b // 5, (b % 5) * NB : (b % 5 + 1) * NB, :]
-        invert_factor(z, w, m11, m)
-        hi, lo = split2(m[...])
+        hi, lo = split2(m_ref[...])
         mh[...], ml[...] = hi, lo
         for b in range(16):
             i, j = b // 4, b % 4
@@ -130,7 +128,7 @@
         mode_ref[:, n : n + 256] = (mm(ah, ph, NT) + mm(ah, plo, NT) + mm(al, ph, NT)) * scale
 
 
-def finish(gram, cross, y, scale):
+def finish(m, cross, y, scale):
     rows = y.shape[0]
     step = rows // 4
     whole = lambda *shape: pl.BlockSpec(shape, lambda i: (0,) * len(shape))
@@ -138,19 +136,12 @@
         functools.partial(finish_kernel, scale),
         grid=(4,),
         out_shape=(jax.ShapeDtypeStruct((K, K), F32), jax.ShapeDtypeStruct((rows, K), F32)),
-        in_specs=[whole(*gram.shape), whole(*cross.shape), pl.BlockSpec((step, K), lambda i: (i, 0))],
+        in_specs=[whole(K, K), whole(*cross.shape), pl.BlockSpec((step, K), lambda i: (i, 0))],
         out_specs=(whole(K, K), pl.BlockSpec((step, K), lambda i: (i, 0))),
-        scratch_shapes=[
-            pltpu.VMEM((K, K), F32),
-            pltpu.VMEM((NB, 2 * NB), F32),
-            pltpu.VMEM((NB, NB), F32),
-            pltpu.VMEM((K, K), F32),
-            pltpu.VMEM((K, K), BF16),
-            pltpu.VMEM((K, K), BF16),
-        ],
+        scratch_shapes=[pltpu.VMEM((K, K), F32), pltpu.VMEM((K, K), BF16), pltpu.VMEM((K, K), BF16)],
         compiler_params=pltpu.CompilerParams(vmem_limit_bytes=60 << 20),
-        name="factor_and_modes",
-    )(gram, cross, y)
+        name="operator_and_modes",
+    )(m, cross, y)
 
 
 GP, CP = 40, 64
@@ -163,8 +154,8 @@
         ref[b // per, (b % per) * NB : (b % per + 1) * NB, :] = value[:, n * NB : (n + 1) * NB]
 
 
-def sums_kernel(x_hbm, y_hbm, g_out, c_out, xv, yv, xh, xl, yh, yl, gloc, cloc, gpart, cpart, gsum, csum, gxy, cxy, gz, cz,
-                gred, in_sem, d_send, d_recv, xy_send, xy_recv, z_send, z_recv, ag_send, ag_recv, e_send, e_recv, c_sem):
+def sums_kernel(x_hbm, y_hbm, m_out, c_out, g_out, z, w, m11, xv, yv, xh, xl, yh, yl, gloc, cloc, gpart, cpart, gsum, csum, gxy, cxy, gz, cz,
+                gred, in_sem, d_send, d_recv, xy_send, xy_recv, z_send, z_recv, ag_send, ag_recv, e_send, e_recv):
     my, mz, mc, mx = [lax.axis_index(a) for a in AXES]
     oc = 1 - mc
     me = my * 4 + mx
@@ -252,16 +243,22 @@
         loads[chunks + i].wait()
         part = slice(i * 256, i * 256 + 256)
         yh[part, :], yl[part, :] = split2(yv[part, :])
-    for i in range(4):
+
+    def cross_band(i):
         h, l = xh[:, i * NB : (i + 1) * NB], xl[:, i * NB : (i + 1) * NB]
         to_blocks(cloc, 4 * i, mm(h, yh[...], T0) + mm(h, yl[...], T0) + mm(l, yh[...], T0))
-    c_d = partner(cloc.at[oc], cpart, 1, (d_send, d_recv))
-    c_d.start()
+
+    cross_band(0)
 
     g_d.wait()
     gsum[...] = gloc[mc] + gpart[...]
     g_xy = scatter_plane(gsum, gxy, GP, 0)
     start(g_xy)
+    cross_band(1)
+    cross_band(2)
+    cross_band(3)
+    c_d = partner(cloc.at[oc], cpart, 1, (d_send, d_recv))
+    c_d.start()
     c_d.wait()
     csum[...] = cloc[mc] + cpart[...]
     c_xy = scatter_plane(csum, cxy, CP, 1)
@@ -277,6 +274,14 @@
                                         device_id=(my, along_z(k + 1), mc, mx), device_id_type=MESH) for k in range(7)]
     start(g_z)
 
+    wait(g_z)
+    total = gz[0]
+    for k in range(1, 8):
+        total = total + gz[k]
+    g_out[mc, pl.ds(pl.multiple_of(me * GP, 8), GP), :] = total
+    g_ag = gather_plane(piece(g_out.at[mc], me, GP), g_out.at[mc], GP, 0)
+    start(g_ag)
+
     wait(c_xy)
     total = csum[pl.ds(pl.multiple_of(me * CP, 8), CP), :]
     for k in range(15):
@@ -286,36 +291,37 @@
                                         device_id=(my, along_z(k + 1), mc, mx), device_id_type=MESH) for k in range(7)]
     start(c_z)
 
-    wait(g_z)
-    total = gz[0]
-    for k in range(1, 8):
-        total = total + gz[k]
-    g_out[mc, pl.ds(pl.multiple_of(me * GP, 8), GP), :] = total
-    g_ag = gather_plane(piece(g_out.at[mc], me, GP), g_out.at[mc], GP, 0)
-    start(g_ag)
+    wait(g_ag)
+    g_e = partner(g_out.at[mc], g_out.at[mc], 0, (e_send, e_recv))
+    g_e.start()
 
     wait(c_z)
     total = csum[pl.ds(pl.multiple_of(mz * 8, 8), 8), :]
     for k in range(7):
         total = total + cz[k]
-    mine = pl.multiple_of(me * CP, 8)
-    c_out[mc, pl.ds(mine + pl.multiple_of(mz * 8, 8), 8), :] = total
-    src = c_out.at[mc, pl.ds(mine + pl.multiple_of(mz * 8, 8), 8), :]
-    c_zg = [pltpu.make_async_remote_copy(src, src, z_send.at[2, k], z_recv.at[2, k],
+    own = pl.ds(pl.multiple_of(me * CP + mz * 8, 8), 8)
+    c_out[mc, own, :] = total
+    c_zg = [pltpu.make_async_remote_copy(c_out.at[mc, own, :], c_out.at[mc, own, :], z_send.at[2, k], z_recv.at[2, k],
                                          device_id=(my, along_z(k + 1), mc, mx), device_id_type=MESH) for k in range(7)]
     start(c_zg)
-
-    wait(g_ag)
-    g_e = partner(g_out.at[mc], g_out.at[mc], 0, (e_send, e_recv))
-    g_e.start()
-
-    wait(c_zg)
     c_ag = gather_plane(piece(c_out.at[mc], me, CP), c_out.at[mc], CP, 1)
-    start(c_ag)
-    wait(c_ag)
     c_e = partner(c_out.at[mc], c_out.at[mc], 1, (e_send, e_recv))
-    c_e.start()
+
+    def between(kb):
+        @pl.when(kb == 1)
+        def _():
+            wait(c_zg)
+            start(c_ag)
+
+        @pl.when(kb == 3)
+        def _():
+            wait(c_ag)
+            c_e.start()
+
     g_e.wait()
+    for b, (i, j) in enumerate(UPPER):
+        z[i * NB : (i + 1) * NB, j * NB : (j + 1) * NB] = g_out[b // 5, (b % 5) * NB : (b % 5 + 1) * NB, :]
+    invert_factor(z, w, m11, m_out, between)
     c_e.wait()
 
 
@@ -326,27 +332,28 @@
     dma = pltpu.SemaphoreType.DMA
     return pl.pallas_call(
         sums_kernel,
-        out_shape=(jax.ShapeDtypeStruct((2, 640, NB), F32), jax.ShapeDtypeStruct((2, 1024, NB), F32)),
+        out_shape=(jax.ShapeDtypeStruct((K, K), F32), jax.ShapeDtypeStruct((2, 1024, NB), F32)),
         in_specs=[pl.BlockSpec(memory_space=pl.ANY)] * 2,
         out_specs=(pl.BlockSpec(memory_space=pltpu.VMEM),) * 2,
         scratch_shapes=[
+            vm((2, 640, NB), F32), vm((K, K), F32), vm((NB, 2 * NB), F32), vm((NB, NB), F32),
             vm((rows, K), F32), vm((rows, K), F32),
             vm((rows, K), BF16), vm((rows, K), BF16), vm((rows, K), BF16), vm((rows, K), BF16),
             vm((2, 640, NB), F32), vm((2, 1024, NB), F32),
             vm((640, NB), F32), vm((1024, NB), F32), vm((640, NB), F32), vm((1024, NB), F32),
             vm((15, GP, NB), F32), vm((15, CP, NB), F32), vm((8, GP, NB), F32), vm((7, 8, NB), F32), vm((GP, NB), F32),
             dma((2 * chunks,)), dma((2,)), dma((2,)), dma((2, 15)), dma((2, 15)), dma((3, 7)), dma((3, 7)),
-            dma((2, 15)), dma((2, 15)), dma((2,)), dma((2,)), dma(()),
+            dma((2, 15)), dma((2, 15)), dma((2,)), dma((2,)),
         ],
         compiler_params=pltpu.CompilerParams(collective_id=0, has_side_effects=True, vmem_limit_bytes=60 << 20),
-        name="products_and_sums",
+        name="sums_and_factor",
     )(x, y)
 
 
 def on_device(first_snaps, next_snaps):
     scale = math.sqrt(first_snaps.shape[0] * lax.axis_size(AXES))
-    gram, cross = sums(first_snaps, next_snaps)
-    return finish(gram, cross, next_snaps, scale)
+    inverse, cross = sums(first_snaps, next_snaps)
+    return finish(inverse, cross, next_snaps, scale)
 
 
 def solution(mesh):

time: 75.9 us -> 67.2 us (0.89)
  Pallas kernels: 75.1 us -> 66.4 us
    pallas_call x1, Pallas kernels: 27 us -> 8.44 us  [finish(): pl.pallas_call(functools.partial(finish_kernel, scale), grid=(4,), out_sh...]
    pallas_call x1, Pallas kernels: 48.2 us -> 58 us  [sums(): pl.pallas_call(sums_kernel, out_shape=(jax.ShapeDtypeStruct((K, K), F32),...]
where the time goes in v1:
time: 67.2 us; the launch traced here: 67 us
  Pallas kernels  66.4 us (99%)
    pallas_call x1, Pallas kernels, sums(): pl.pallas_call(sums_kernel, out_shape=(jax.ShapeDtypeStruct((K, K), F32),...  58 us
    pallas_call x1, Pallas kernels, finish(): pl.pallas_call(functools.partial(finish_kernel, scale), grid=(4,), out_sh...  8.44 us

profile of v1, /device:TPU:1, one launch (start us, length us, event | category | flops | bytes accessed | tf_op | source)
XLA Modules:
  0.0 67.0 jit_solution(10671641218529035656)
XLA Ops:
  0.6 58.0 %sums_and_factor.1 = (f32[512,512]{1,0:T(8,128)}, f32[2,1024,128]{2,1,0:T(8,128)}) custom-call(f32[1792,512]{1,0:T(8,128)} %x_hbm.1, f32[1792,512]{1,0:T(8,128)} %y_ref.1), custom_call_target="tpu_custom_call" | custom-call | tf_op jit(solution)/shard_map/sums_and_factor/pallas_call | solution.py:333
  58.6 8.4 %operator_and_modes.1 = (f32[512,512]{1,0:T(8,128)}, f32[1792,512]{1,0:T(8,128)}) custom-call(f32[512,512]{1,0:T(8,128)} %get-tuple-element.4.m_ref, f32[2,1024,128]{2,1,0:T(8,128)} %get-tuple-element.5.c_ref, f32[1792,512]{1,0:T(8,128)} %y_ref.1), custom_call_target="tpu_custom_call" | custom-call | tf_op jit(solution)/shard_map/operator_and_modes/pallas_call | solution.py:135

commit v2 on v1

v2 whole, which is shorter than its diff:
```python
import functools
import math

import jax
import jax.numpy as jnp
from jax import lax
from jax.experimental import pallas as pl
from jax.experimental.pallas import tpu as pltpu
from jax.sharding import Mesh
from jax.sharding import PartitionSpec as P

AXES = ("y", "z", "c", "x")
MESH = pl.DeviceIdType.MESH
K = 512
NB = 128
F32, BF16 = jnp.float32, jnp.bfloat16
T0 = (((0,), (0,)), ((), ()))
NN = (((1,), (0,)), ((), ()))
NT = (((1,), (1,)), ((), ()))
GROUPS = (
    [(0, j) for j in range(4)],
    [(i, j) for i in range(1, 4) for j in range(i, 4)],
    [(i, j) for i in range(4) for j in range(4)],
)
HALF = [len(blocks) * NB // 2 for blocks in GROUPS]
PIECE = [rows // 16 for rows in HALF]


def split2(x):
    hi = x.astype(BF16)
    return hi, (x - hi.astype(F32)).astype(BF16)


def split3(x):
    hi = x.astype(BF16)
    rest = x - hi.astype(F32)
    mid = rest.astype(BF16)
    return hi, mid, (rest - mid.astype(F32)).astype(BF16)


def mm(a, b, dims):
    return lax.dot_general(a, b, dims, preferred_element_type=F32)


def lane_splat(v, lane):
    return jnp.broadcast_to(v[:, lane : lane + 1], v.shape)


def row_splat(v, row):
    return jnp.broadcast_to(v[row : row + 1, :], v.shape)


def eliminate_block(w, out, midway):
    sub = lax.broadcasted_iota(jnp.int32, (8, NB), 0)
    for t in range(NB // 8):
        if t == 8:
            midway()
        r0 = 8 * t
        pa, pb = w[r0 : r0 + 8, :NB], w[r0 : r0 + 8, NB:]
        s = [lane_splat(pa, r0 + j) for j in range(8)]
        rs, uas, ubs, ums = [], [], [], []
        for j in range(8):
            r = lax.rsqrt(row_splat(s[j], j))
            low = jnp.where(sub > j, s[j] * r, 0.0)
            ua, ub = row_splat(pa, j) * r, row_splat(pb, j) * r
            um = {m: row_splat(s[m], j) * r for m in range(j + 1, 8)}
            for m in um:
                s[m] = s[m] - low * um[m]
            pa, pb = pa - low * ua, pb - low * ub
            out[r0 + j : r0 + j + 1, :] = ub[0:1, :]
            rs.append(r), uas.append(ua), ubs.append(ub), ums.append(um)
        for g in range(t + 1, NB // 8):
            rows = slice(8 * g, 8 * g + 8)
            wa, wb = w[rows, :NB], w[rows, NB:]
            sg = [lane_splat(wa, r0 + j) for j in range(8)]
            for j in range(8):
                low = sg[j] * rs[j]
                for m in range(j + 1, 8):
                    sg[m] = sg[m] - low * ums[j][m]
                wa, wb = wa - low * uas[j], wb - low * ubs[j]
            w[rows, :NB], w[rows, NB:] = wa, wb


def dot6(a3, b3, dims):
    ca, cb = dims[0][0][0], dims[0][1][0]
    ah, am, al = a3
    bh, bm, bl = b3
    left = jnp.concatenate([ah, ah, am, ah, al, am], axis=ca)
    right = jnp.concatenate([bh, bm, bh, bl, bh, bm], axis=cb)
    return mm(left, right, dims)


def invert_factor(z, w, m11, m, midway, after):
    eye = jnp.where(
        lax.broadcasted_iota(jnp.int32, (NB, NB), 0) == lax.broadcasted_iota(jnp.int32, (NB, NB), 1), 1.0, 0.0
    ).astype(F32)
    cols = lax.broadcasted_iota(jnp.int32, (NB, K), 1)
    wide = lax.broadcasted_iota(jnp.int32, (K, K), 1)

    def block_step(kb, carry):
        c0 = pl.multiple_of(kb * NB, NB)
        c1 = c0 + NB
        rows = pl.ds(c0, NB)
        w[:, :NB] = z[rows, rows]
        w[:, NB:] = eye
        eliminate_block(w, m11, lambda: midway(kb))
        z[rows, rows] = eye
        t = dot6(split3(m11[...]), split3(z[rows, :]), NN)
        m[rows, :] = jnp.where(cols < c1, t, 0.0)
        after(kb)

        @pl.when(kb < K // NB - 1)
        def _():
            update = dot6(split3(jnp.where(cols >= c1, t, 0.0)), split3(t), T0)
            z[...] = jnp.where((wide >= c0) & (wide < c1), 0.0, z[...]) - update

        return carry

    lax.fori_loop(0, K // NB, block_step, 0)


def finish_kernel(scale, m_ref, c_ref, modes_ref, red_ref, out_ref, z, sem):
    copy = pltpu.make_async_copy(modes_ref, out_ref, sem)
    copy.start()
    unpack(z, c_ref, 2)
    hi, lo = split2(m_ref[...])
    ch, cl = split2(z[...])
    lh, ll = split2(mm(hi, ch, NN) + mm(hi, cl, NN) + mm(lo, ch, NN))
    red_ref[...] = (mm(lh, hi, NT) + mm(lh, lo, NT) + mm(ll, hi, NT)) * scale
    copy.wait()


def finish(m, cross, modes, scale):
    in_vmem = pl.BlockSpec(memory_space=pltpu.VMEM)
    anywhere = pl.BlockSpec(memory_space=pl.ANY)
    return pl.pallas_call(
        functools.partial(finish_kernel, scale),
        out_shape=(jax.ShapeDtypeStruct((K, K), F32), jax.ShapeDtypeStruct(modes.shape, F32)),
        in_specs=[in_vmem, in_vmem, anywhere],
        out_specs=(in_vmem, anywhere),
        scratch_shapes=[pltpu.VMEM((K, K), F32), pltpu.SemaphoreType.DMA(())],
        compiler_params=pltpu.CompilerParams(vmem_limit_bytes=24 << 20),
        name="operator",
    )(m, cross, modes)


def place(ref, group, i, first, value):
    per = ref.shape[1] // NB
    for n in range(value.shape[1] // NB):
        b = GROUPS[group].index((i, first + n))
        ref[b // per, (b % per) * NB : (b % per + 1) * NB, :] = value[:, n * NB : (n + 1) * NB]


def unpack(z, ref, group):
    per = ref.shape[1] // NB
    for b, (i, j) in enumerate(GROUPS[group]):
        z[i * NB : (i + 1) * NB, j * NB : (j + 1) * NB] = ref[b // per, (b % per) * NB : (b % per + 1) * NB, :]


def sums_kernel(scale, x_hbm, y_hbm, m_out, c_out, mode_out, mh, ml, z, w, m11, xv, yv, xh, xl, yh, yl, g0_out, g1_out,
                loc0, loc1, loc2, other0, other1, other2, chip0, chip1, chip2, land0, land1, cland1, cland2, cpart, cown, mine0, mine1,
                lz0, lz1, lz2, in_sem, d_send, d_recv, xy_send, xy_recv, z_send, z_recv, ag_send, ag_recv, e_send, e_recv,
                c_send, c_recv, f_send, f_recv):
    my, mz, mc, mx = [lax.axis_index(a) for a in AXES]
    oc = 1 - mc
    me = my * 4 + mx
    chunks = xv.shape[0] // 256
    loc, other, chip, land = (loc0, loc1, loc2), (other0, other1, other2), (chip0, chip1, chip2), (land0, land1)
    out = (g0_out, g1_out)
    plane = [(dy, dx) for dy in range(4) for dx in range(4)][1:]

    loads = []
    for n, (src, dst) in enumerate(((x_hbm, xv), (y_hbm, yv))):
        for i in range(chunks):
            part = pl.ds(i * 256, 256)
            loads.append(pltpu.make_async_copy(src.at[part], dst.at[part], in_sem.at[n * chunks + i]))
    for load in loads:
        load.start()

    def in_plane(dy, dx):
        return lax.rem(my + dy + 4, 4), lax.rem(mx + dx + 4, 4)

    def along_z(dz):
        return lax.rem(mz + dz, 8)

    barrier = pltpu.get_barrier_semaphore()
    pl.semaphore_signal(barrier, inc=1, device_id=(my, mz, oc, mx), device_id_type=MESH)
    for dy, dx in plane:
        py, px = in_plane(dy, dx)
        pl.semaphore_signal(barrier, inc=1, device_id=(py, mz, mc, px), device_id_type=MESH)
    for dz in range(1, 8):
        pl.semaphore_signal(barrier, inc=1, device_id=(my, along_z(dz), mc, mx), device_id_type=MESH)

    def piece(ref, who, size):
        return ref.at[pl.ds(pl.multiple_of(who * size, 8), size), :]

    def to_partner(src, dst, sends, recvs):
        return pltpu.make_async_remote_copy(src, dst, sends, recvs, device_id=(my, mz, oc, mx), device_id_type=MESH)

    def to_plane(src, dst, k, sends, recvs):
        py, px = in_plane(*plane[k])
        return pltpu.make_async_remote_copy(src, dst, sends, recvs, device_id=(py, mz, mc, px), device_id_type=MESH)

    def to_z(src, dst, k, sends, recvs):
        return pltpu.make_async_remote_copy(src, dst, sends, recvs, device_id=(my, along_z(k + 1), mc, mx), device_id_type=MESH)

    def start(copies):
        for c in copies:
            c.start()
        return copies

    def wait(copies):
        for c in copies:
            c.wait()

    def pair(n):
        return start([to_partner(loc[n].at[oc], other[n], d_send.at[n], d_recv.at[n])])

    def scatter(n, copies):
        wait(copies)
        chip[n][...] = loc[n][mc] + other[n][...]
        made = []
        for k in range(15):
            py, px = in_plane(*plane[k])
            made.append(to_plane(piece(chip[n], py * 4 + px, PIECE[n]), land[n].at[k], k, xy_send.at[n, k], xy_recv.at[n, k]))
        return start(made)

    def plane_sum(n, copies):
        wait(copies)
        total = chip[n][pl.ds(pl.multiple_of(me * PIECE[n], 8), PIECE[n]), :]
        for k in range(15):
            total = total + land[n][k]
        return total

    def spread_z(n, copies):
        mine, lz = ((mine0, lz0), (mine1, lz1))[n]
        total = plane_sum(n, copies)
        mine[...] = total
        lz[mz] = total
        return start([to_z(mine, lz.at[mz], k, z_send.at[n, k], z_recv.at[n, k]) for k in range(7)])

    def gather_plane(n):
        mine = piece(out[n].at[mc], me, PIECE[n])
        made = start([to_plane(mine, mine, k, ag_send.at[n, k], ag_recv.at[n, k]) for k in range(15)])
        return made, start([to_partner(mine, mine, e_send.at[n, 15], e_recv.at[n, 15])])

    def gather(n, copies):
        lz = (lz0, lz1)[n]
        wait(copies)
        total = lz[0]
        for k in range(1, 8):
            total = total + lz[k]
        out[n][mc, pl.ds(pl.multiple_of(me * PIECE[n], 8), PIECE[n]), :] = total
        return gather_plane(n)

    def pass_on(n, state):
        made, sent = state
        for k, (dy, dx) in enumerate(plane):
            made[k].wait_recv()
            py, px = in_plane(-dy, -dx)
            landed = piece(out[n].at[mc], py * 4 + px, PIECE[n])
            sent = sent + start([to_partner(landed, landed, e_send.at[n, k], e_recv.at[n, k])])
        for c in made:
            c.wait_send()
        return sent

    a_rows = lambda x, y: x * NB + y * 32
    b_rows = lambda y, x: HALF[2] // 2 + y * NB + x * 32

    def line(half, along_x, d):
        return (my, mz, mc, lax.rem(mx + d + 4, 4)) if along_x else (lax.rem(my + d + 4, 4), mz, mc, mx)

    def on_line(stage, half, along_x, d, src, dst):
        return pltpu.make_async_remote_copy(src, dst, c_send.at[stage, half, d - 1], c_recv.at[stage, half, d - 1],
                                            device_id=line(half, along_x, d), device_id_type=MESH)

    def aligned(ref, first, size):
        return ref.at[pl.ds(pl.multiple_of(first, 8), size), :]

    def cross_first(copies):
        wait(copies)
        chip2[...] = loc2[mc] + other2[...]
        made = []
        for d in (1, 2, 3):
            made.append(on_line(0, 0, True, d, aligned(chip2, a_rows(lax.rem(mx + d, 4), 0), NB), cland1.at[0, d - 1]))
            made.append(on_line(0, 1, False, d, aligned(chip2, b_rows(lax.rem(my + d, 4), 0), NB), cland1.at[1, d - 1]))
        return start(made)

    def cross_second(copies):
        wait(copies)
        for half, first in ((0, a_rows(mx, 0)), (1, b_rows(my, 0))):
            cpart[half] = chip2[pl.ds(pl.multiple_of(first, 8), NB), :] + cland1[half, 0] + cland1[half, 1] + cland1[half, 2]
        made = []
        for d in (1, 2, 3):
            made.append(on_line(1, 0, False, d, aligned(cpart.at[0], lax.rem(my + d, 4) * 32, 32), cland2.at[0, d - 1]))
            made.append(on_line(1, 1, True, d, aligned(cpart.at[1], lax.rem(mx + d, 4) * 32, 32), cland2.at[1, d - 1]))
        return start(made)

    def cross_z(copies):
        wait(copies)
        for half, first in ((0, my * 32), (1, mx * 32)):
            cown[half * 32 : half * 32 + 32, :] = (
                cpart[half, pl.ds(pl.multiple_of(first, 8), 32), :] + cland2[half, 0] + cland2[half, 1] + cland2[half, 2]
            )

    upper = mz // 4
    own = pl.ds(pl.multiple_of((1 - upper) * a_rows(mx, my) + upper * b_rows(my, mx) + lax.rem(mz, 4) * 8, 8), 8)

    def cross_back(copies):
        wait(copies)
        total = cown[pl.ds(pl.multiple_of(mz * 8, 8), 8), :]
        for k in range(7):
            total = total + lz2[k]
        c_out[mc, own, :] = total

    def cross_lines(stage, size, swap):
        made = []
        for d in (1, 2, 3):
            for half, first in ((0, a_rows(mx, 0 if swap else my)), (1, b_rows(my, 0 if swap else mx))):
                rows = aligned(c_out.at[mc], first, size)
                made.append(on_line(stage, half, (half == 0) == swap, d, rows, rows))
        return made

    def cross_forwards():
        made = [(0, a_rows(mx, 0)), (4, b_rows(my, 0))]
        for d in (1, 2, 3):
            made += [(d, a_rows(lax.rem(mx - d + 4, 4), 0)), (4 + d, b_rows(lax.rem(my - d + 4, 4), 0))]
        return [to_partner(aligned(c_out.at[mc], first, NB), aligned(c_out.at[mc], first, NB), f_send.at[k], f_recv.at[k])
                for k, first in made]

    for i in range(chunks):
        loads[i].wait()
        part = slice(i * 256, i * 256 + 256)
        xh[part, :], xl[part, :] = split2(xv[part, :])

    def gram_band(c0, c1):
        h, l, h2, l2 = xh[:, c0:c1], xl[:, c0:c1], xh[:, c0:], xl[:, c0:]
        return mm(h, h2, T0) + mm(h, l2, T0) + mm(l, h2, T0) + mm(l, l2, T0)

    place(loc0, 0, 0, 0, gram_band(0, NB))
    pl.semaphore_wait(barrier, 1 + len(plane) + 7)
    g0 = pair(0)
    place(loc1, 1, 1, 1, gram_band(NB, 2 * NB))
    g = gram_band(2 * NB, K)
    place(loc1, 1, 2, 2, g[:NB])
    place(loc1, 1, 3, 3, g[NB:, NB:])
    g1 = pair(1)
    g0 = scatter(0, g0)
    for i in range(chunks):
        loads[chunks + i].wait()
        part = slice(i * 256, i * 256 + 256)
        yh[part, :], yl[part, :] = split2(yv[part, :])
    g1 = scatter(1, g1)
    def cross_bands(bands):
        for i in bands:
            h, l = xh[:, i * NB : (i + 1) * NB], xl[:, i * NB : (i + 1) * NB]
            place(loc2, 2, i, 0, mm(h, yh[...], T0) + mm(h, yl[...], T0) + mm(l, yh[...], T0))

    cross_bands((0, 1))
    g0 = spread_z(0, g0)
    cross_bands((2, 3))
    c = pair(2)
    g1 = spread_z(1, g1)
    c = cross_first(c)
    g0 = gather(0, g0)
    g1 = gather(1, g1)
    c = cross_second(c)
    g0 = pass_on(0, g0)
    c_over = [to_z(piece(cown, along_z(k + 1), 8), lz2.at[k], k, z_send.at[2, k], z_recv.at[2, k]) for k in range(7)]
    c_rows = c_out.at[mc, own, :]
    c_back = [to_z(c_rows, c_rows, k, z_send.at[3, k], z_recv.at[3, k]) for k in range(7)]
    c_third = cross_lines(2, 32, False)
    c_fourth = cross_lines(3, NB, True)
    c_sent = cross_forwards()

    def awaited(n):
        copies = []
        for k, (dy, dx) in enumerate(plane):
            py, px = in_plane(-dy, -dx)
            landed = piece(out[n].at[mc], py * 4 + px, PIECE[n])
            copies.append(to_partner(landed, landed, e_send.at[n, k], e_recv.at[n, k]))
        mine = piece(out[n].at[mc], me, PIECE[n])
        return copies + [to_partner(mine, mine, e_send.at[n, 15], e_recv.at[n, 15])]

    def midway(kb):
        @pl.when(kb == 0)
        def _():
            pass_on(1, g1)
            cross_z(c)
            start(c_over)

        @pl.when(kb == 1)
        def _():
            cross_back(c_over)
            start(c_back)

        @pl.when(kb == 2)
        def _():
            wait(c_back)
            start(c_third)

    def after(kb):
        @pl.when(kb == 0)
        def _():
            wait(awaited(1))
            unpack(z, g1_out, 1)

        @pl.when(kb == 2)
        def _():
            wait(c_third)
            start(c_fourth)
            start(c_sent[:2])

    wait(g0)
    unpack(z, g0_out, 0)
    invert_factor(z, w, m11, m_out, midway, after)

    mh[...], ml[...] = split2(m_out[...])

    def modes(i, carry):
        rows = pl.ds(pl.multiple_of(i * 256, 256), 256)
        for n, k1 in ((0, 256), (256, 512)):
            ph, plo = mh[n : n + 256, :k1], ml[n : n + 256, :k1]
            ah, al = yh[rows, :k1], yl[rows, :k1]
            mode_out[rows, n : n + 256] = (mm(ah, ph, NT) + mm(ah, plo, NT) + mm(al, ph, NT)) * scale
        @pl.when(i == 1)
        def _():
            for k, copy in enumerate(c_fourth):
                copy.wait_recv()
                c_sent[2 + k].start()
            for copy in c_fourth:
                copy.wait_send()

        return carry

    lax.fori_loop(0, chunks, modes, 0)
    wait(c_sent)


def sums(x, y, scale):
    rows = x.shape[0]
    vm = pltpu.VMEM
    dma = pltpu.SemaphoreType.DMA
    per_group = lambda lead, sizes: [vm((*lead, size, NB), F32) for size in sizes]
    return pl.pallas_call(
        functools.partial(sums_kernel, scale),
        out_shape=(
            jax.ShapeDtypeStruct((K, K), F32),
            jax.ShapeDtypeStruct((2, HALF[2], NB), F32),
            jax.ShapeDtypeStruct((rows, K), F32),
        ),
        in_specs=[pl.BlockSpec(memory_space=pltpu.MemorySpace.HBM)] * 2,
        out_specs=(pl.BlockSpec(memory_space=pltpu.VMEM),) * 3,
        scratch_shapes=[
            vm((K, K), BF16), vm((K, K), BF16),
            vm((K, K), F32), vm((NB, 2 * NB), F32), vm((NB, NB), F32),
            vm((rows, K), F32), vm((rows, K), F32),
            vm((rows, K), BF16), vm((rows, K), BF16), vm((rows, K), BF16), vm((rows, K), BF16),
            *per_group((2,), HALF[:2]),
            *per_group((2,), HALF), *per_group((), HALF), *per_group((), HALF), *per_group((15,), PIECE[:2]),
            vm((2, 3, NB, NB), F32), vm((2, 3, 32, NB), F32), vm((2, NB, NB), F32), vm((64, NB), F32),
            *per_group((), PIECE[:2]), *per_group((8,), PIECE[:2]), vm((7, 8, NB), F32),
            dma((2 * (rows // 256),)), dma((3,)), dma((3,)), dma((2, 15)), dma((2, 15)), dma((4, 7)), dma((4, 7)),
            dma((2, 15)), dma((2, 15)), dma((2, 16)), dma((2, 16)), dma((4, 2, 3)), dma((4, 2, 3)), dma((8,)), dma((8,)),
        ],
        compiler_params=pltpu.CompilerParams(collective_id=0, has_side_effects=True, vmem_limit_bytes=32 << 20),
        name="sums_and_factor",
    )(x, y)


def on_device(first_snaps, next_snaps):
    scale = math.sqrt(first_snaps.shape[0] * lax.axis_size(AXES))
    hbm = pltpu.MemorySpace.HBM
    in_hbm = [pltpu.with_memory_space_constraint(a, hbm) for a in (first_snaps, next_snaps)]
    inverse, cross, modes = sums(*in_hbm, scale)
    return finish(inverse, cross, modes, scale)


def solution(mesh):
    finer = Mesh(mesh.devices.reshape(4, 8, 2, 4), AXES)
    spec = P(AXES, None)
    return jax.shard_map(
        on_device, mesh=finer, in_specs=(spec, spec), out_specs=(P(), spec), check_vma=False
    )
```

time: 67.2 us -> 62.5 us (0.930)
  Pallas kernels: 66.4 us -> 61.7 us
    pallas_call x2, Pallas kernels: 66.4 us -> 61.7 us  [the longest x1 58.8 us: sums(): pl.pallas_call(functools.partial(sums_kernel, scale), out_shape=(jax.Shap...]
where the time goes in v2:
time: 62.5 us
  Pallas kernels  61.7 us (99%)
  between operations  0.8 us (1%)
    pallas_call x1, Pallas kernels, sums(): pl.pallas_call(functools.partial(sums_kernel, scale), out_shape=(jax.Shap...  58.8 us
    pallas_call x1, Pallas kernels, finish(): pl.pallas_call(functools.partial(finish_kernel, scale), out_shape=(jax.Sh...  2.86 us

profile of v2, /device:TPU:1, one launch (start us, length us, event | category | flops | bytes accessed | tf_op | source)
XLA Modules:
  0.0 62.5 jit_solution(16290242188748395839)
XLA Ops:
  0.6 58.8 %sums_and_factor.1 = (f32[512,512]{1,0:T(8,128)S(1)}, f32[2,1024,128]{2,1,0:T(8,128)S(1)}, f32[1792,512]{1,0:T(8,128)S(1)}) custom-call(f32[1792,512]{1,0:T(8,128)} %x_hbm.1, f32[1792,512]{1,0:T(8,128)} %y_hbm.1), custom_call_target="tpu_custom_call" | custom-call | tf_op jit(solution)/shard_map/sums_and_factor/pallas_call | solution.py:445
  59.4 2.9 %operator.1 = (f32[512,512]{1,0:T(8,128)}, f32[1792,512]{1,0:T(8,128)}) custom-call(f32[512,512]{1,0:T(8,128)S(1)} %get-tuple-element.5.m_ref, f32[2,1024,128]{2,1,0:T(8,128)S(1)} %get-tuple-element.6.c_ref, f32[1792,512]{1,0:T(8,128)S(1)} %get-tuple-element.7.modes_ref), custom_call_target="tpu_custom_call" | custom-call | tf_op jit(solution)/shard_map/operator/pallas_call | solution.py:136

commit v3 on v2

--- a/solution.py
+++ b/solution.py
@@ -52,33 +52,53 @@
 
 def eliminate_block(w, out, midway):
     sub = lax.broadcasted_iota(jnp.int32, (8, NB), 0)
+    lane = lax.broadcasted_iota(jnp.int32, (8, NB), 1)
+    p = w[0:8, :]
+    s = [lane_splat(p, j) for j in range(8)]
     for t in range(NB // 8):
         if t == 8:
             midway()
         r0 = 8 * t
-        pa, pb = w[r0 : r0 + 8, :NB], w[r0 : r0 + 8, NB:]
-        s = [lane_splat(pa, r0 + j) for j in range(8)]
-        rs, uas, ubs, ums = [], [], [], []
+        more = t + 1 < NB // 8
+        inside = (lane >= r0) & (lane < r0 + 8)
+        p = jnp.where(inside, jnp.where(sub == lane - r0, 1.0, 0.0), p)
+        if more:
+            na = w[r0 + 8 : r0 + 16, :]
+            nn = [lane_splat(na, r0 + j) for j in range(8)]
+            nx = [lane_splat(na, r0 + 8 + m) for m in range(8)]
+            na = jnp.where(inside, 0.0, na)
+        rs, us, ums, done = [], [], [], p
         for j in range(8):
             r = lax.rsqrt(row_splat(s[j], j))
             low = jnp.where(sub > j, s[j] * r, 0.0)
-            ua, ub = row_splat(pa, j) * r, row_splat(pb, j) * r
             um = {m: row_splat(s[m], j) * r for m in range(j + 1, 8)}
             for m in um:
                 s[m] = s[m] - low * um[m]
-            pa, pb = pa - low * ua, pb - low * ub
-            out[r0 + j : r0 + j + 1, :] = ub[0:1, :]
-            rs.append(r), uas.append(ua), ubs.append(ub), ums.append(um)
-        for g in range(t + 1, NB // 8):
+            u = row_splat(p, j) * r
+            p = p - low * u
+            done = jnp.where(sub == j, u, done)
+            if more:
+                ln = nn[j] * r
+                for m in um:
+                    nn[m] = nn[m] - ln * um[m]
+                na = na - ln * u
+                for m in range(8):
+                    nx[m] = nx[m] - ln * row_splat(ln, m)
+            rs.append(r), us.append(u), ums.append(um)
+        out[r0 : r0 + 8, :] = jnp.where(lane < r0 + 8, done, 0.0)
+        for g in range(t + 2, NB // 8):
             rows = slice(8 * g, 8 * g + 8)
-            wa, wb = w[rows, :NB], w[rows, NB:]
+            wa = w[rows, :]
             sg = [lane_splat(wa, r0 + j) for j in range(8)]
+            wa = jnp.where(inside, 0.0, wa)
             for j in range(8):
                 low = sg[j] * rs[j]
                 for m in range(j + 1, 8):
                     sg[m] = sg[m] - low * ums[j][m]
-                wa, wb = wa - low * uas[j], wb - low * ubs[j]
-            w[rows, :NB], w[rows, NB:] = wa, wb
+                wa = wa - low * us[j]
+            w[rows, :] = wa
+        if more:
+            p, s = na, nx
 
 
 def dot6(a3, b3, dims):
@@ -101,8 +121,7 @@
         c0 = pl.multiple_of(kb * NB, NB)
         c1 = c0 + NB
         rows = pl.ds(c0, NB)
-        w[:, :NB] = z[rows, rows]
-        w[:, NB:] = eye
+        w[...] = z[rows, rows]
         eliminate_block(w, m11, lambda: midway(kb))
         z[rows, rows] = eye
         t = dot6(split3(m11[...]), split3(z[rows, :]), NN)
@@ -351,20 +370,23 @@
         part = slice(i * 256, i * 256 + 256)
         yh[part, :], yl[part, :] = split2(yv[part, :])
     g1 = scatter(1, g1)
-    def cross_bands(bands):
-        for i in bands:
-            h, l = xh[:, i * NB : (i + 1) * NB], xl[:, i * NB : (i + 1) * NB]
-            place(loc2, 2, i, 0, mm(h, yh[...], T0) + mm(h, yl[...], T0) + mm(l, yh[...], T0))
-
-    cross_bands((0, 1))
+    def cross_half(half):
+        for i in range(2):
+            band = pl.ds(pl.multiple_of((half * 2 + i) * NB, NB), NB)
+            h, l = xh[:, band], xl[:, band]
+            value = mm(h, yh[...], T0) + mm(h, yl[...], T0) + mm(l, yh[...], T0)
+            for j in range(4):
+                loc2[half, (4 * i + j) * NB : (4 * i + j + 1) * NB, :] = value[:, j * NB : (j + 1) * NB]
+
+    cross_half(oc)
+    c = pair(2)
     g0 = spread_z(0, g0)
-    cross_bands((2, 3))
-    c = pair(2)
+    cross_half(mc)
+    c = cross_first(c)
     g1 = spread_z(1, g1)
-    c = cross_first(c)
     g0 = gather(0, g0)
+    c = cross_second(c)
     g1 = gather(1, g1)
-    c = cross_second(c)
     g0 = pass_on(0, g0)
     c_over = [to_z(piece(cown, along_z(k + 1), 8), lz2.at[k], k, z_send.at[2, k], z_recv.at[2, k]) for k in range(7)]
     c_rows = c_out.at[mc, own, :]
@@ -386,31 +408,28 @@
         @pl.when(kb == 0)
         def _():
             pass_on(1, g1)
-            cross_z(c)
-            start(c_over)
-
-        @pl.when(kb == 1)
-        def _():
-            cross_back(c_over)
-            start(c_back)
 
         @pl.when(kb == 2)
         def _():
             wait(c_back)
             start(c_third)
+
+        @pl.when(kb == 3)
+        def _():
+            wait(c_third)
+            start(c_fourth)
+            start(c_sent[:2])
 
     def after(kb):
         @pl.when(kb == 0)
         def _():
             wait(awaited(1))
             unpack(z, g1_out, 1)
-
-        @pl.when(kb == 2)
-        def _():
-            wait(c_third)
-            start(c_fourth)
-            start(c_sent[:2])
-
+            cross_back(c_over)
+            start(c_back)
+
+    cross_z(c)
+    start(c_over)
     wait(g0)
     unpack(z, g0_out, 0)
     invert_factor(z, w, m11, m_out, midway, after)
@@ -423,17 +442,14 @@
             ph, plo = mh[n : n + 256, :k1], ml[n : n + 256, :k1]
             ah, al = yh[rows, :k1], yl[rows, :k1]
             mode_out[rows, n : n + 256] = (mm(ah, ph, NT) + mm(ah, plo, NT) + mm(al, ph, NT)) * scale
-        @pl.when(i == 1)
-        def _():
-            for k, copy in enumerate(c_fourth):
-                copy.wait_recv()
-                c_sent[2 + k].start()
-            for copy in c_fourth:
-                copy.wait_send()
-
         return carry
 
     lax.fori_loop(0, chunks, modes, 0)
+    for k, copy in enumerate(c_fourth):
+        copy.wait_recv()
+        c_sent[2 + k].start()
+    for copy in c_fourth:
+        copy.wait_send()
     wait(c_sent)
 
 
@@ -453,7 +469,7 @@
         out_specs=(pl.BlockSpec(memory_space=pltpu.VMEM),) * 3,
         scratch_shapes=[
             vm((K, K), BF16), vm((K, K), BF16),
-            vm((K, K), F32), vm((NB, 2 * NB), F32), vm((NB, NB), F32),
+            vm((K, K), F32), vm((NB, NB), F32), vm((NB, NB), F32),
             vm((rows, K), F32), vm((rows, K), F32),
             vm((rows, K), BF16), vm((rows, K), BF16), vm((rows, K), BF16), vm((rows, K), BF16),
             *per_group((2,), HALF[:2]),

time: 62.5 us -> 59 us (0.944)
  Pallas kernels: 61.7 us -> 58.1 us
    pallas_call x1, Pallas kernels: 58.8 us -> 55.3 us  [sums(): pl.pallas_call(functools.partial(sums_kernel, scale), out_shape=(jax.Shap...]
where the time goes in v3:
time: 59 us; the launch traced here: 58.9 us
  Pallas kernels  58.1 us (98%)
  between operations  0.8 us (1%)
    pallas_call x1, Pallas kernels, sums(): pl.pallas_call(functools.partial(sums_kernel, scale), out_shape=(jax.Shap...  55.3 us
    pallas_call x1, Pallas kernels, finish(): pl.pallas_call(functools.partial(finish_kernel, scale), out_shape=(jax.Sh...  2.86 us

profile of v3, /device:TPU:1, one launch (start us, length us, event | category | flops | bytes accessed | tf_op | source)
XLA Modules:
  0.0 58.9 jit_solution(9168345275348114709)
XLA Ops:
  0.6 55.3 %sums_and_factor.1 = (f32[512,512]{1,0:T(8,128)S(1)}, f32[2,1024,128]{2,1,0:T(8,128)S(1)}, f32[1792,512]{1,0:T(8,128)S(1)}) custom-call(f32[1792,512]{1,0:T(8,128)} %x_hbm.1, f32[1792,512]{1,0:T(8,128)} %y_hbm.1), custom_call_target="tpu_custom_call" | custom-call | tf_op jit(solution)/shard_map/sums_and_factor/pallas_call | solution.py:461
  55.9 2.9 %operator.1 = (f32[512,512]{1,0:T(8,128)}, f32[1792,512]{1,0:T(8,128)}) custom-call(f32[512,512]{1,0:T(8,128)S(1)} %get-tuple-element.5.m_ref, f32[2,1024,128]{2,1,0:T(8,128)S(1)} %get-tuple-element.6.c_ref, f32[1792,512]{1,0:T(8,128)S(1)} %get-tuple-element.7.modes_ref), custom_call_target="tpu_custom_call" | custom-call | tf_op jit(solution)/shard_map/operator/pallas_call | solution.py:155

commit v4 on v3

--- a/solution.py
+++ b/solution.py
@@ -144,8 +144,13 @@
     unpack(z, c_ref, 2)
     hi, lo = split2(m_ref[...])
     ch, cl = split2(z[...])
-    lh, ll = split2(mm(hi, ch, NN) + mm(hi, cl, NN) + mm(lo, ch, NN))
-    red_ref[...] = (mm(lh, hi, NT) + mm(lh, lo, NT) + mm(ll, hi, NT)) * scale
+    for n, k1 in ((0, 256), (256, 512)):
+        h, l, ah, al = hi[n : n + 256, :k1], lo[n : n + 256, :k1], ch[:k1], cl[:k1]
+        z[n : n + 256, :] = mm(h, ah, NN) + mm(h, al, NN) + mm(l, ah, NN)
+    lh, ll = split2(z[...])
+    for n, k1 in ((0, 256), (256, 512)):
+        h, l, ah, al = hi[n : n + 256, :k1], lo[n : n + 256, :k1], lh[:, :k1], ll[:, :k1]
+        red_ref[:, n : n + 256] = (mm(ah, h, NT) + mm(ah, l, NT) + mm(al, h, NT)) * scale
     copy.wait()
 
 
@@ -442,14 +447,18 @@
             ph, plo = mh[n : n + 256, :k1], ml[n : n + 256, :k1]
             ah, al = yh[rows, :k1], yl[rows, :k1]
             mode_out[rows, n : n + 256] = (mm(ah, ph, NT) + mm(ah, plo, NT) + mm(al, ph, NT)) * scale
+
+        @pl.when(i == 4)
+        def _():
+            for k, copy in enumerate(c_fourth):
+                copy.wait_recv()
+                c_sent[2 + k].start()
+            for copy in c_fourth:
+                copy.wait_send()
+
         return carry
 
     lax.fori_loop(0, chunks, modes, 0)
-    for k, copy in enumerate(c_fourth):
-        copy.wait_recv()
-        c_sent[2 + k].start()
-    for copy in c_fourth:
-        copy.wait_send()
     wait(c_sent)
 
 

time: 59 us -> 58.6 us (level)
  no operation moved by 1% of the time
where the time goes in v4:
time: 58.6 us
  Pallas kernels  57.8 us (99%)
  between operations  0.8 us (1%)
    pallas_call x1, Pallas kernels, sums(): pl.pallas_call(functools.partial(sums_kernel, scale), out_shape=(jax.Shap...  54.9 us
    pallas_call x1, Pallas kernels, finish(): pl.pallas_call(functools.partial(finish_kernel, scale), out_shape=(jax.Sh...  2.86 us

profile of v4, /device:TPU:1, one launch (start us, length us, event | category | flops | bytes accessed | tf_op | source)
XLA Modules:
  0.0 58.6 jit_solution(12524976377309514090)
XLA Ops:
  0.6 54.9 %sums_and_factor.1 = (f32[512,512]{1,0:T(8,128)S(1)}, f32[2,1024,128]{2,1,0:T(8,128)S(1)}, f32[1792,512]{1,0:T(8,128)S(1)}) custom-call(f32[1792,512]{1,0:T(8,128)} %x_hbm.1, f32[1792,512]{1,0:T(8,128)} %y_hbm.1), custom_call_target="tpu_custom_call" | custom-call | tf_op jit(solution)/shard_map/sums_and_factor/pallas_call | solution.py:470
  55.5 2.9 %operator.1 = (f32[512,512]{1,0:T(8,128)}, f32[1792,512]{1,0:T(8,128)}) custom-call(f32[512,512]{1,0:T(8,128)S(1)} %get-tuple-element.5.m_ref, f32[2,1024,128]{2,1,0:T(8,128)S(1)} %get-tuple-element.6.c_ref, f32[1792,512]{1,0:T(8,128)S(1)} %get-tuple-element.7.modes_ref), custom_call_target="tpu_custom_call" | custom-call | tf_op jit(solution)/shard_map/operator/pallas_call | solution.py:160
